TPU v7x, 256 devices: a whole 4x4x8 slice. The times are simulated.
256 devices in a mesh: seq: 2 (over core), chan: 16 (over y, x), batch: 8 (over z).
Axes of the slice: x: 4, y: 4, z: 8, core: 2. Of those that a mesh axis runs over, the one named last changes fastest.
Arguments:
- ssm_input: bfloat16 [16384, 4096], P(('batch', 'seq'), 'chan'), parts along dimension 0, may hold values from -6 to 6
- gate_z: bfloat16 [16384, 4096], P(('batch', 'seq'), 'chan'), parts along dimension 0, may hold values from -6 to 6
- proj_forward: bfloat16 [2, 16384, 128], P(None, ('batch', 'seq')), parts along dimension 1, may hold values from -2 to 2
- proj_backward: bfloat16 [2, 16384, 128], P(None, ('batch', 'seq')), parts along dimension 1, may hold values from -2 to 2
- step_raw: float32 [2, 64, 16384], P(None, 'chan', ('batch', 'seq')), parts along dimension 2, may hold values from -3 to 3
- head_params: float32 [2, 2, 64], P(None, None, 'chan'), may hold values from -4 to 1, as said below
- skip_gain: float32 [64], P('chan'), may hold values from 0.25 to 2
- norm_gain: float32 [4096], P('chan'), may hold values from 0.5 to 1.5
- out_weight: bfloat16 [4096, 2048], P(None, 'chan'), may hold values from -0.09375 to 0.09375
Outputs:
- mixed: bfloat16 [16384, 2048], P(('batch', 'seq'), 'chan'), parts along dimension 0
There are 8 independent parts, one for each index of `batch`. A program takes and returns all parts, laid end to end along the dimension named above; an argument that names none is the same for every part. Nothing has to cross between parts.
Inputs may be any that keep to these rules, and one draw needn't show every extreme that they name: `head_params`: index 0 of the second dimension holds positive decay rates, index 1 time-step biases.
All inputs are finite; a program needn't handle non-finite values.
Results may differ from a plain program's by a relative error of at most 0.0085.
Values may be sent and summed in bfloat16 or wider, within the bound.
A program may use at most 128 MiB of HBM per device.

v0:
```python
import jax
import jax.numpy as jnp
from jax import lax
from jax.sharding import PartitionSpec as P

SPAN = 256
INNER = 4096


def sent_together(arrays, axis, dim, along):
    columns = [a.reshape(*a.shape[:along], -1) for a in arrays]
    both = jnp.concatenate(columns, axis=along)
    whole, at, done = (lax.all_gather(both, axis, axis=dim, tiled=True), 0, [])
    for a, column in zip(arrays, columns):
        slab = whole[..., at : at + column.shape[along]]
        done.append(slab.reshape(*slab.shape[:along], *a.shape[along:]))
        at += column.shape[along]
    return tuple(done)


def copy_for_each(value, axis):
    copies = jnp.broadcast_to(value, (lax.axis_size(axis), *value.shape))
    return lax.all_to_all(copies, axis, split_axis=0, concat_axis=0, tiled=True)


def taken_together(value, axis):
    everything = copy_for_each(value, axis)
    return jnp.sum(everything, axis=0)


def local_scan(blocks_x, b_rows, c_rows, steps_here, decay_rates):
    cumlog = jnp.cumsum(-decay_rates[None, :, None] * steps_here, axis=2)
    scores = jnp.einsum("cqn,csn->cqs", c_rows, b_rows, preferred_element_type=jnp.float32)
    lower_mask = jnp.tril(jnp.ones((SPAN, SPAN), dtype=bool))
    log_gaps = cumlog[:, :, :, None] - cumlog[:, :, None, :]
    decays = jnp.where(lower_mask, jnp.exp(jnp.where(lower_mask, log_gaps, 0.0)), 0.0)
    weights = (scores[:, None] * decays * steps_here[:, :, None, :]).astype(jnp.bfloat16)
    intra_out = jnp.einsum("chts,cshp->cthp", weights, blocks_x, preferred_element_type=jnp.float32)
    end_logs = cumlog[:, :, -1]
    in_weights = jnp.exp(end_logs[:, :, None] - cumlog) * steps_here
    b_weighted = (b_rows[:, None].astype(jnp.float32) * in_weights[..., None]).astype(jnp.bfloat16)
    block_states = jnp.einsum(
        "cshp,chsn->chpn", blocks_x, b_weighted, preferred_element_type=jnp.float32
    )

    def advance(carried, inputs):
        gain_log, block_state = inputs
        return (jnp.exp(gain_log)[:, None, None] * carried + block_state, carried)

    initial = jnp.zeros(block_states.shape[1:], jnp.float32)
    end_state, entering = lax.scan(advance, initial, (end_logs, block_states))
    before = jnp.cumsum(end_logs, axis=0) - end_logs
    whole_decay = jnp.exp(jnp.sum(end_logs, axis=0))
    return ((intra_out, entering, cumlog, before, c_rows), (whole_decay, end_state))


def finish(pieces, carried):
    intra_out, entering, cumlog, before, c_rows = pieces
    states = entering + jnp.exp(before)[:, :, None, None] * carried[None]
    inter = jnp.einsum("ctn,chpn->cthp", c_rows.astype(jnp.float32), states)
    inter = inter * jnp.exp(cumlog).transpose(0, 2, 1)[..., None]
    outputs = intra_out + inter
    return outputs.reshape(outputs.shape[0] * outputs.shape[1], -1)


def body(
    ssm_input,
    gate_z,
    proj_forward,
    proj_backward,
    step_raw,
    head_params,
    skip_gain,
    norm_gain,
    out_weight,
):
    frames, inner_here = ssm_input.shape
    heads_here = step_raw.shape[1]
    width = inner_here // heads_here
    blocks = frames // SPAN
    shape_x = (blocks, SPAN, heads_here, width)
    shape_rows = (blocks, SPAN, proj_forward.shape[2])

    def to_blocks(steps):
        return steps.reshape(heads_here, blocks, SPAN).transpose(1, 0, 2)

    steps_fwd = jax.nn.softplus(step_raw[0] + head_params[0, 1][:, None])
    steps_bwd = jax.nn.softplus(step_raw[1] + head_params[1, 1][:, None])[:, ::-1]
    fwd_parts, fwd_end = local_scan(
        ssm_input.reshape(shape_x),
        proj_forward[0].reshape(shape_rows),
        proj_forward[1].reshape(shape_rows),
        to_blocks(steps_fwd),
        head_params[0, 0],
    )
    bwd_parts, bwd_end = local_scan(
        ssm_input[::-1].reshape(shape_x),
        proj_backward[0][::-1].reshape(shape_rows),
        proj_backward[1][::-1].reshape(shape_rows),
        to_blocks(steps_bwd),
        head_params[1, 0],
    )
    decays_all, states_all = tuple(
        (
            part.astype(jnp.float32)
            for part in sent_together(
                (
                    jnp.stack([fwd_end[0], bwd_end[0]])[None].astype(jnp.bfloat16),
                    jnp.stack([fwd_end[1], bwd_end[1]])[None].astype(jnp.bfloat16),
                ),
                "seq",
                0,
                3,
            )
        )
    )
    own_index = lax.axis_index("seq")
    group_size = lax.axis_size("seq")

    def accumulate(position, carried):
        forward_state, backward_state = carried
        mirror = group_size - 1 - position
        forward_state = jnp.where(
            position < own_index,
            decays_all[position, 0][:, None, None] * forward_state + states_all[position, 0],
            forward_state,
        )
        backward_state = jnp.where(
            mirror > own_index,
            decays_all[mirror, 1][:, None, None] * backward_state + states_all[mirror, 1],
            backward_state,
        )
        return (forward_state, backward_state)

    empty_state = jnp.zeros(fwd_end[1].shape, jnp.float32)
    carry_fwd, carry_bwd = lax.fori_loop(0, group_size, accumulate, (empty_state, empty_state))
    forward_out = finish(fwd_parts, carry_fwd)
    backward_out = finish(bwd_parts, carry_bwd)[::-1]
    skipped = (
        ssm_input.reshape(frames, heads_here, width).astype(jnp.float32) * skip_gain[:, None]
    ).reshape(frames, inner_here)
    gated = (forward_out + backward_out + skipped) * jax.nn.silu(gate_z.astype(jnp.float32))
    squares = taken_together(jnp.sum(gated * gated, axis=1), "chan")
    scale = lax.rsqrt(squares / INNER + 1.0)
    normed = (gated * scale[:, None] * norm_gain).astype(jnp.bfloat16)
    frame_share = lax.all_to_all(normed, "chan", split_axis=0, concat_axis=1, tiled=True)
    projected = jnp.dot(
        frame_share,
        lax.all_gather(out_weight, "chan", axis=1, tiled=True),
        preferred_element_type=jnp.float32,
    ).astype(jnp.bfloat16)
    return lax.all_to_all(projected, "chan", split_axis=1, concat_axis=0, tiled=True)


def solution(mesh):
    in_specs = (
        P(("batch", "seq"), "chan"),
        P(("batch", "seq"), "chan"),
        P(None, ("batch", "seq"), None),
        P(None, ("batch", "seq"), None),
        P(None, "chan", ("batch", "seq")),
        P(None, None, "chan"),
        P("chan"),
        P("chan"),
        P(None, "chan"),
    )
    out_specs = P(("batch", "seq"), "chan")
    return jax.shard_map(body, mesh=mesh, in_specs=in_specs, out_specs=out_specs, check_vma=False)
```

profile of v0, /device:TPU:32, one launch (start us, length us, event | category | flops | bytes accessed | tf_op | source)
XLA Modules:
  0.0 171.0 jit_solution(11320585137728651989)
XLA Ops:
  6.5 0.7 all-gather.2.cloned.1.call-update
  7.3 1.2 copy.167
  8.5 6.3 %rev.17 = bf16[1024,256]{1,0:T(8,128)(2,1)S(1)} reverse(bf16[1024,256]{1,0:T(8,128)(2,1)} %param.15), dimensions={0} | reverse | bytes 1048576 | tf_op jit(solution)/shard_map/rev | solution.py:97
  14.9 0.7 slice.57
  15.6 0.8 negate_bitcast_fusion
  16.4 0.8 compare_select_fusion
  17.2 0.7 rev.15
  18.0 4.8 %reduce-window.14 = f32[4,4,2,128]{3,2,1,0:T(2,128)S(1)} reduce-window(f32[4,4,2,128]{3,2,1,0:T(2,128)S(1)} %reshape.296, f32[]{:T(128)} %constant.83.clone.1), window={size=1x1x1x128 pad=0_0x0_0x0_0x127_0}, to_apply=%region_0.1 | reduce-window | flops 520192 | bytes 32772 | tf_op jit(solution)/shard_map/reduce-window
  23.0 0.1 copy.165
  23.1 0.1 copy.166
  23.4 0.2 slice_reduce_fusion.1
  23.5 0.1 copy.192
  23.6 1.1 fusion.56
  24.8 1.2 reshape.298
  26.0 0.6 exponential_multiply_fusion.1
  26.6 1.9 %convolution_bitcast_fusion.3 = f32[4,4,64,128]{3,2,1,0:T(8,128)S(1)} fusion(f32[4,4,256]{2,1,0:T(4,128)S(1)} %get-tuple-element.329, f32[4,256,128]{2,1,0:T(8,128)S(1)} %convert_element_type.76, bf16[4,256,4,64]{1,0,3,2:T(4,128)(2,1)} %reshape.298), kind=kOutput, calls=%fused_computation.48 | convolution fusion | flops 68157440 | bytes 1589248 | tf_op jit(solution)/shard_map/cshp,chsn->chpn/dot_general | solution.py:42
  28.6 0.6 while.44
  29.2 4.8 %reduce-window.16 = f32[4,4,2,128]{3,2,1,0:T(2,128)S(1)} reduce-window(f32[4,4,2,128]{3,2,1,0:T(2,128)S(1)} %reshape.300, f32[]{:T(128)} %constant.83.clone.1), window={size=1x1x1x128 pad=0_0x0_0x0_0x127_0}, to_apply=%region_6.7 | reduce-window | flops 520192 | bytes 32772 | tf_op jit(solution)/shard_map/reduce-window.2
  34.2 0.1 copy.172
  34.3 0.1 copy.173
  34.4 0.1 broadcast_add_fusion
  34.6 0.2 slice_reduce_fusion
  34.7 0.1 copy.193
  34.9 1.8 %slice_bitcast_fusion = (bf16[1024,128]{1,0:T(8,128)(2,1)}, bf16[1024,128]{1,0:T(8,128)(2,1)S(1)}) fusion(bf16[2,1024,128]{2,1,0:T(8,128)(2,1)} %param.18), kind=kLoop, calls=%fused_computation.70 | loop fusion | bytes 1048576 | tf_op jit(solution)/shard_map/squeeze | solution.py:99
  36.6 0.3 rev.16
  36.9 0.8 convert_element_type.78
  37.7 0.4 reshape.310
  38.1 0.5 copy.176
  38.7 0.6 exponential_bitcast_fusion
  39.3 2.0 %convolution_bitcast_fusion.2 = f32[4,4,64,128]{3,2,1,0:T(8,128)S(1)} fusion(bf16[4,256,4,64]{1,3,2,0:T(8,128)(2,1)S(1)} %copy.176, f32[4,4,256]{2,1,0:T(4,128)S(1)} %get-tuple-element.324, f32[4,256,128]{2,1,0:T(8,128)} %convert_element_type.78), kind=kOutput, calls=%fused_computation.47 | convolution fusion | flops 68157440 | bytes 1589248 | tf_op jit(solution)/shard_map/cshp,chsn->chpn/dot_general | solution.py:42
  41.3 0.6 while.45
  42.0 0.1 copy.177
  42.2 0.1 maximum_maximum_fusion
  42.3 0.4 copy-done.2
  42.7 2.0 %all_gather.6 = bf16[2,2,4,8193]{3,2,1,0:T(4,128)(2,1)S(1)} all-gather(bf16[1,2,4,8193]{3,2,1,0:T(4,128)(2,1)S(1)} %maximum_maximum_fusion), channel_id=1, replica_groups=mesh['seq'=2,'chan'=16,'batch'=8] {'seq'}, dimensions={0}, use_global_device_ids=true | all-gather | bytes 393264 | tf_op jit(solution)/shard_map/all_gather | solution.py:13
  44.7 0.2 slice_convert_fusion
  44.9 0.4 reshape.307
  45.3 3.2 %rev.18 = bf16[1024,128]{1,0:T(8,128)(2,1)S(1)} reverse(bf16[1024,128]{1,0:T(8,128)(2,1)} %get-tuple-element.319), dimensions={0} | reverse | bytes 524288 | tf_op jit(solution)/shard_map/rev | solution.py:99
  48.6 0.6 subtract_exponential_fusion
  49.2 0.3 fusion.58
  49.6 3.1 %fusion.22 = f32[4,256,4,64]{1,3,2,0:T(8,128)} fusion(bf16[4,256,4,64]{1,3,2,0:T(8,128)(2,1)S(1)} %copy.176, f32[4,4,256]{2,1,0:T(4,128)} %bitcast.166, f32[4,4,256]{2,1,0:T(4,128)S(1)} %copy-done.9, f32[4,256,256]{2,1,0:T(8,128)S(1)} %fusion.58, pred[256,256]{1,0:T(8,128)(4,1)S(1)} %iota_compare_fusion), kind=kOutput, calls=%fused_computation.37 | convolution fusion | flops 140509184 | bytes 2719744 | tf_op jit(solution)/shard_map/chts,cshp->cthp/dot_general | solution.py:38
  52.7 0.3 while.46
  52.7 0.1 fusion.76
  52.9 0.1 fusion.76
  53.0 0.7 copy-done.3
  53.7 1.6 fusion.25
  55.4 0.7 copy.180
  56.0 0.2 copy.199
  56.3 1.5 rev.19
  57.8 0.3 fusion.57
  58.2 2.5 %fusion.23 = f32[4,256,4,64]{1,3,2,0:T(8,128)S(1)} fusion(f32[4,4,256]{2,1,0:T(4,128)S(1)} %copy-done.13, f32[4,4,256]{2,1,0:T(4,128)S(1)} %copy-done.7, f32[4,256,256]{2,1,0:T(8,128)S(1)} %fusion.57, pred[256,256]{1,0:T(8,128)(4,1)S(1)} %copy-done.11, bf16[4,256,4,64]{1,0,3,2:T(4,128)(2,1)} %reshape.298), kind=kOutput, calls=%fused_computation.38 | convolution fusion | flops 140509184 | bytes 2719744 | tf_op jit(solution)/shard_map/chts,cshp->cthp/dot_general | solution.py:38
  60.7 0.3 fusion.27
  61.1 0.7 copy.178
  61.8 1.2 copy.198
  62.9 0.2 copy.182
  63.3 1.8 %multiply_reduce_fusion = (f32[1024]{0:T(1024)S(1)}, f32[1024,256]{0,1:T(8,128)S(1)}) fusion(bf16[1024,256]{0,1:T(8,128)(2,1)S(1)} %copy.182, f32[256]{0:T(256)S(1)} %mul.274, bf16[1024,256]{0,1:T(8,128)(2,1)S(1)} %copy.167, f32[1024,256]{0,1:T(8,128)} %bitcast.150, f32[1024,256]{0,1:T(8,128)S(1)} %rev.19), kind=kLoop, calls=%fused_computation.55 | loop fusion | flops 3144704 | bytes 4199424 | tf_op jit(solution)/shard_map/reduce_sum | solution.py:143
  65.2 15.2 %all_to_all.46 = f32[16,1,1024]{2,1,0:T(1,128)S(1)} all-to-all(f32[16,1,1024]{2,1,0:T(1,128)S(1)} %broadcast_in_dim.57), channel_id=1, replica_groups=mesh['seq'=2,'chan'=16,'batch'=8] {'chan'}, dimensions={0} | all-to-all | bytes 131072 | tf_op jit(solution)/shard_map/all_to_all | solution.py:23
  80.5 0.1 multiply_convert_fusion.12
  80.6 0.2 copy.184
  80.8 16.7 %all_to_all.44 = bf16[16,64,256]{2,1,0:T(8,128)(2,1)S(1)} all-to-all(bf16[16,64,256]{2,1,0:T(8,128)(2,1)S(1)} %bitcast.160), channel_id=1, replica_groups=mesh['seq'=2,'chan'=16,'batch'=8] {'chan'}, dimensions={0} | all-to-all | bytes 1048576 | tf_op jit(solution)/shard_map/all_to_all | solution.py:146
  97.5 43.7 %all-gather.2.cloned.1.call-done = bf16[4096,2048]{1,0:T(8,128)(2,1)} async-done(((bf16[4096,128]{1,0:T(8,128)(2,1)}), bf16[4096,2048]{1,0:T(8,128)(2,1)}) %all-gather.2.cloned.1.call-update) | async-done | bytes 16777232 | tf_op jit(solution)/shard_map/all_gather | solution.py:149
  141.2 8.8 %fusion.28 = bf16[8,16,8,128]{3,2,1,0:T(8,128)(2,1)S(1)} fusion(bf16[64,4096]{1,0:T(8,128)(2,1)S(1)} %bitcast.151, bf16[4096,2048]{1,0:T(8,128)(2,1)} %all-gather.2.cloned.1.call-done), kind=kOutput, calls=%fused_computation.49 | convolution fusion | flops 1073872896 | bytes 17563648 | tf_op jit(solution)/shard_map/dot_general | solution.py:147
  150.0 13.4 %all_to_all.45 = bf16[64,16,128]{2,0,1:T(8,128)(2,1)S(1)} all-to-all(bf16[64,16,128]{2,0,1:T(8,128)(2,1)S(1)} %bitcast.162), channel_id=1, replica_groups=mesh['seq'=2,'chan'=16,'batch'=8] {'chan'}, dimensions={1} | all-to-all | bytes 524288 | tf_op jit(solution)/shard_map/all_to_all | solution.py:152
  163.4 0.7 copy.241
  (103 shorter events, 2.2 us)
Async XLA Ops:
  6.5 134.6 %all-gather.2.cloned.1.call-start = ((), (), s32[]{:S(2)}) async-start(), calls=%async_computation.3 | async-start | bytes 17825792 | tf_op jit(solution)/shard_map/all_gather | solution.py:149
  17.9 20.8 %copy-start.5 = (f32[4,1024]{1,0:T(4,128)}, f32[4,1024]{1,0:T(4,128)S(1)}, u32[]{:S(2)}) copy-start(f32[4,1024]{1,0:T(4,128)S(1)} %rev.15) | copy-start | bytes 49156
  18.0 10.5 %copy-start.12 = (f32[4,4,256]{2,1,0:T(4,128)}, f32[4,4,256]{2,1,0:T(4,128)S(1)}, u32[]{:S(2)}) copy-start(f32[4,4,256]{2,1,0:T(4,128)S(1)} %get-tuple-element.314) | copy-start | bytes 49156
  23.3 3.3 %copy-start.6 = (f32[4,4,256]{2,1,0:T(4,128)}, f32[4,4,256]{2,1,0:T(4,128)S(1)}, u32[]{:S(2)}) copy-start(f32[4,4,256]{2,1,0:T(4,128)S(1)} %reduce_window_sum.59) | copy-start | bytes 49156
  29.2 7.5 %copy-start = (f32[4,4,64,128]{3,2,1,0:T(8,128)}, f32[4,4,64,128]{3,2,1,0:T(8,128)S(1)}, u32[]{:S(2)}) copy-start(f32[4,4,64,128]{3,2,1,0:T(8,128)S(1)} %get-tuple-element.216) | copy-start | bytes 1572868
  29.2 7.7 %copy-start.16 = (f32[4,4]{1,0:T(4,128)}, f32[4,4]{1,0:T(4,128)S(1)}, u32[]{:S(2)}) copy-start(f32[4,4]{1,0:T(4,128)S(1)} %get-tuple-element.516) | copy-start | bytes 196
  34.5 6.8 %copy-start.8 = (f32[4,4,256]{2,1,0:T(4,128)}, f32[4,4,256]{2,1,0:T(4,128)S(1)}, u32[]{:S(2)}) copy-start(f32[4,4,256]{2,1,0:T(4,128)S(1)} %reduce_window_sum.62) | copy-start | bytes 49156
  41.9 0.8 copy-start.2
  42.0 7.6 %copy-start.9 = (f32[4,4,256]{2,1,0:T(4,128)S(1)}, f32[4,4,256]{2,1,0:T(4,128)}, u32[]{:S(2)}) copy-start(f32[4,4,256]{2,1,0:T(4,128)} %copy-done.8) | copy-start | bytes 49156
  48.6 4.1 %copy-start.10 = (pred[256,256]{1,0:T(8,128)(4,1)}, pred[256,256]{1,0:T(8,128)(4,1)S(1)}, u32[]{:S(2)}) copy-start(pred[256,256]{1,0:T(8,128)(4,1)S(1)} %iota_compare_fusion) | copy-start | bytes 196612
  52.7 1.0 copy-start.3
  52.7 1.0 copy-start.15
  55.3 2.4 %copy-start.17 = (f32[4,4]{1,0:T(4,128)S(1)}, f32[4,4]{1,0:T(4,128)}, u32[]{:S(2)}) copy-start(f32[4,4]{1,0:T(4,128)} %copy-done.16) | copy-start | bytes 196
  55.3 2.8 %copy-start.7 = (f32[4,4,256]{2,1,0:T(4,128)S(1)}, f32[4,4,256]{2,1,0:T(4,128)}, u32[]{:S(2)}) copy-start(f32[4,4,256]{2,1,0:T(4,128)} %copy-done.6) | copy-start | bytes 49156
  55.3 2.8 %copy-start.11 = (pred[256,256]{1,0:T(8,128)(4,1)S(1)}, pred[256,256]{1,0:T(8,128)(4,1)}, u32[]{:S(2)}) copy-start(pred[256,256]{1,0:T(8,128)(4,1)} %copy-done.10) | copy-start | bytes 196612
  55.4 2.8 %copy-start.13 = (f32[4,4,256]{2,1,0:T(4,128)S(1)}, f32[4,4,256]{2,1,0:T(4,128)}, u32[]{:S(2)}) copy-start(f32[4,4,256]{2,1,0:T(4,128)} %copy-done.12) | copy-start | bytes 49156
  58.1 2.5 %copy-start.1 = (f32[4,4,64,128]{3,2,1,0:T(8,128)S(1)}, f32[4,4,64,128]{3,2,1,0:T(8,128)}, u32[]{:S(2)}) copy-start(f32[4,4,64,128]{3,2,1,0:T(8,128)} %copy-done) | copy-start | bytes 1572868
  58.2 2.5 %copy-start.14 = (f32[4,256,4]{1,2,0:T(4,128)S(1)}, f32[4,256,4]{1,2,0:T(4,128)}, u32[]{:S(2)}) copy-start(f32[4,256,4]{1,2,0:T(4,128)} %get-tuple-element.330) | copy-start | bytes 49156
  60.7 2.3 %copy-start.4 = (bf16[1024,256]{1,0:T(8,128)(2,1)S(1)}, bf16[1024,256]{1,0:T(8,128)(2,1)}, u32[]{:S(2)}) copy-start(bf16[1024,256]{1,0:T(8,128)(2,1)} %param.16) | copy-start | bytes 1572868
  60.7 2.5 %copy-start.19 = (f32[4]{0:T(128)S(1)}, f32[4]{0:T(128)}, u32[]{:S(2)}) copy-start(f32[4]{0:T(128)} %param.21) | copy-start | bytes 52
  61.7 18.7 %copy-start.18 = (f32[256]{0:T(256)S(1)}, f32[256]{0:T(256)}, u32[]{:S(2)}) copy-start(f32[256]{0:T(256)} %param.22) | copy-start | bytes 3076
Sparse Core Ops, SparseCore 0:
  9.7 131.4 all-gather.1
where the time goes:
time: 173 us; the launch traced here: 171 us
  blocking collectives  47.2 us (27%)
  waiting for transfers between devices  44.4 us (26%)
  local copies, waits for them, and re-layouts  26 us (15%)
  matrix products  20.8 us (12%)
  other arithmetic  18.2 us (11%)
  between operations  14 us (8%)
    all_gather x1, waiting for transfers between devices, body(): lax.all_gather(out_weight, 'chan', axis=1, tiled=True)  43.7 us
    all_to_all x1, blocking collectives, body(): lax.all_to_all(normed, 'chan', split_axis=0, concat_axis=1, tiled=True)  16.7 us
    all_to_all x1, blocking collectives, copy_for_each(): return lax.all_to_all(copies, axis, split_axis=0, concat_axis=0, tiled=True)  15.2 us
    all_to_all x1, blocking collectives, body(): lax.all_to_all(projected, 'chan', split_axis=1, concat_axis=0, tiled=True)  13.4 us
    another operation x8, other arithmetic  9.89 us
    dot_general x1, matrix products, body(): jnp.dot(frame_share, lax.all_gather(out_weight, 'chan', axis=1, tiled=Tru...  8.79 us
    rev x1, local copies, waits for them, and re-layouts, body(): ssm_input[::-1].reshape(shape_x)  6.33 us
    dot_general x2, matrix products, local_scan(): jnp.einsum('chts,cshp->cthp', weights, blocks_x, preferred_element_type=j...  5.62 us
  transfers between devices with their start and end apart: 1, of which 1 were waited for; matrix products, arithmetic and copies ran while one was open for 32% of the time, Pallas kernels for 0%

commit v1 on v0

v1 whole, which is shorter than its diff:
```python
import jax
import jax.numpy as jnp
from jax import lax
from jax.experimental import pallas as pl
from jax.experimental.pallas import tpu as pltpu
from jax.sharding import PartitionSpec as P

MESH = pl.DeviceIdType.MESH
F32, BF16 = jnp.float32, jnp.bfloat16
SPAN = 256
HALF = 128
BLOCKS = 4
HEADS = 4
WIDE = 256
SIDE = 4
COLS = 128
NST = 128
INNER = 4096
LOG2E = 1.4426950408889634


def iota(shape, dim):
    return lax.broadcasted_iota(jnp.int32, shape, dim)


def dot(a, b):
    return jnp.dot(a, b, preferred_element_type=F32)


def dot_tt(a, b):
    return lax.dot_general(a, b, (((0,), (0,)), ((), ())), preferred_element_type=F32)


def dot_nt(a, b):
    return lax.dot_general(a, b, (((1,), (1,)), ((), ())), preferred_element_type=F32)


def split(v, parts):
    out = []
    for _ in range(parts - 1):
        high = v.astype(BF16).astype(F32)
        out.append(high)
        v = v - high
    out.append(v)
    return out


def kernel(
    x_hbm, z_hbm, pf_hbm, pb_hbm, st_hbm, hp, skip, gain_ref, w_hbm, out_ref,
    xv, zv, pfv, pbv, stv, w1, w2, a1, a2, os1, os2, or1, or2, ss1, ss2, so1, so2,
    expc, yv, sf, sb, ef, eb, payload, carry,
    in_sem, w_send, w_recv, st_send, st_recv, a_send, a_recv, s_send, s_recv,
    o_send, o_recv, t_send, t_recv,
):
    seq = lax.axis_index("seq")
    chan = lax.axis_index("chan")
    my_y, my_x = chan // SIDE, lax.rem(chan, SIDE)

    loads = []
    for i, (src, dst) in enumerate(
        ((st_hbm, stv), (x_hbm, xv), (pf_hbm, pfv), (pb_hbm, pbv), (z_hbm, zv))
    ):
        copy = pltpu.make_async_copy(src, dst, in_sem.at[i])
        copy.start()
        loads.append(copy)
    def tile(i):
        return pl.ds(pl.multiple_of(i * COLS, COLS), COLS)

    own_w1 = pltpu.make_async_copy(w_hbm.at[:, my_x], w1.at[:, :, tile(my_x)], in_sem.at[5])
    own_w2 = pltpu.make_async_copy(w_hbm.at[my_y], w2.at[:, :, tile(my_y)], in_sem.at[6])
    own_w1.start()
    own_w2.start()

    barrier = pltpu.get_barrier_semaphore()
    ys = [lax.rem(my_y + k, SIDE) for k in range(1, SIDE)]
    xs = [lax.rem(my_x + k, SIDE) for k in range(1, SIDE)]
    to_y = [{"chan": v * SIDE + my_x} for v in ys]
    to_x = [{"chan": my_y * SIDE + v} for v in xs]
    other = {"seq": 1 - seq}
    for dev in to_y + to_x + [other]:
        pl.semaphore_signal(barrier, inc=1, device_id=dev, device_id_type=MESH)
    pl.semaphore_wait(barrier, 7)

    def remote(src, dst, send, recv, dev):
        return pltpu.make_async_remote_copy(
            src_ref=src, dst_ref=dst, send_sem=send, recv_sem=recv,
            device_id=dev, device_id_type=MESH,
        )

    sends = []

    def start(*args):
        copy = remote(*args)
        copy.start()
        sends.append(copy)

    for k in range(3):
        start(w_hbm.at[:, xs[k]], w1.at[:, :, tile(my_x)], w_send.at[0, k], w_recv.at[0, my_x], to_x[k])
        start(w_hbm.at[ys[k]], w2.at[:, :, tile(my_y)], w_send.at[1, k], w_recv.at[1, my_y], to_y[k])

    loads[0].wait()
    row8 = iota((8, BLOCKS * SPAN), 0)
    bias = jnp.zeros((8, BLOCKS * SPAN), F32)
    rate = jnp.zeros((8, BLOCKS * SPAN), F32)
    for j in range(8):
        bias = jnp.where(row8 == j, hp[j // 4, 1, j % 4], bias)
        rate = jnp.where(row8 == j, hp[j // 4, 0, j % 4], rate)
    raw = jnp.concatenate([stv[0], stv[1]], axis=0) + bias
    dt_all = jnp.maximum(raw, 0.0) + jnp.log1p(jnp.exp(-jnp.abs(raw)))
    logs = split(-rate * dt_all, 3)
    stacked = jnp.concatenate(
        [part[:, b * SPAN : (b + 1) * SPAN] for b in range(BLOCKS) for part in logs], axis=0
    ).astype(BF16)
    t_of, s_of = iota((SPAN, SPAN), 0), iota((SPAN, SPAN), 1)
    after = t_of >= s_of
    up_to = dot(stacked, jnp.where(t_of <= s_of, 1.0, 0.0).astype(BF16))
    down_to = dot(stacked, jnp.where(after, 1.0, 0.0).astype(BF16))
    row = iota((8, SPAN), 0)
    is_fwd = row < HEADS

    sel_row, sel_col = iota((16, 2 * WIDE), 0), iota((16, 2 * WIDE), 1)
    spread = jnp.where((sel_row & 7) == (sel_col >> 6), 1.0, 0.0).astype(BF16)
    col_row, col_col = iota((32, 128), 0), iota((32, 128), 1)
    pick = jnp.where(((col_row & 7) == col_col) & (col_row < 24), 1.0, 0.0).astype(BF16)
    zero8 = jnp.zeros((8, SPAN), F32)

    cum2, cprime, dts, decays = [], [], [], []
    for copy in loads[1:4]:
        copy.wait()
    for b in range(BLOCKS):
        at = b * 24
        c_f = up_to[at : at + 8] + up_to[at + 8 : at + 16] + up_to[at + 16 : at + 24]
        c_b = down_to[at : at + 8] + down_to[at + 8 : at + 16] + down_to[at + 16 : at + 24]
        cum = jnp.where(is_fwd, c_f, c_b)
        end = jnp.where(is_fwd, cum[:, SPAN - 1 : SPAN], cum[:, 0:1])
        dt = dt_all[:, b * SPAN : (b + 1) * SPAN]
        e = jnp.exp(cum)
        w = jnp.exp(end - cum) * dt
        c2 = cum * LOG2E
        cum2.append(c2)
        cprime.append(c2 - jnp.log2(dt))
        dts.append(dt)
        e_cols = dot_tt(jnp.concatenate(split(e, 2), axis=0).astype(BF16), spread)
        w_cols = dot_tt(jnp.concatenate(split(w, 2), axis=0).astype(BF16), spread)
        expc[b] = e_cols
        decays.append((e_cols[SPAN - 1 : SPAN, :WIDE], e_cols[0:1, WIDE:]))
        xb = xv[b * SPAN : (b + 1) * SPAN, :].astype(F32)
        sf[b] = dot_tt(pfv[0, b * SPAN : (b + 1) * SPAN, :], (xb * w_cols[:, :WIDE]).astype(BF16))
        sb[b] = dot_tt(pbv[0, b * SPAN : (b + 1) * SPAN, :], (xb * w_cols[:, WIDE:]).astype(BF16))

    end_f = sf[0]
    for b in range(1, BLOCKS):
        end_f = decays[b][0] * end_f + sf[b]
    end_b = sb[BLOCKS - 1]
    for b in reversed(range(BLOCKS - 1)):
        end_b = decays[b][1] * end_b + sb[b]
    payload[...] = jnp.where(seq == 0, end_f, end_b)
    start(payload, carry, st_send.at[0], st_recv.at[0], other)

    lane = iota((SPAN, 128), 1)
    chan_row = iota((1, WIDE), 1) >> 6
    skip_row = jnp.zeros((1, WIDE), F32)
    for h in range(HEADS):
        skip_row = jnp.where(chan_row == h, skip[h], skip_row)
    for b in range(BLOCKS):
        rows = slice(b * SPAN, (b + 1) * SPAN)
        b_f, c_f = pfv[0, rows, :], pfv[1, rows, :]
        b_b, c_b = pbv[0, rows, :], pbv[1, rows, :]
        scores = jnp.where(after, dot_nt(c_f, b_f), dot_nt(c_b, b_b))
        cols = dot_tt(jnp.concatenate(split(cum2[b], 3) + [zero8], axis=0).astype(BF16), pick)
        dt_cols = dot_tt(jnp.concatenate(split(dts[b], 2), axis=0).astype(BF16), spread[:, WIDE:])
        xb = xv[rows, :]
        same = jnp.sum(c_b.astype(F32) * b_b.astype(F32), axis=1, keepdims=True)
        rest = xb.astype(F32) * (same * dt_cols + skip_row)
        for pair in range(2):
            halves = []
            for h in (2 * pair, 2 * pair + 1):
                gaps = jnp.where(
                    after,
                    cols[:, h : h + 1] - cprime[b][h : h + 1, :],
                    cols[:, 4 + h : 5 + h] - cprime[b][4 + h : 5 + h, :],
                )
                weights = (scores * jnp.exp2(gaps)).astype(BF16)
                halves.append(dot(weights, xb[:, pair * 128 : (pair + 1) * 128]))
            lanes = slice(pair * 128, (pair + 1) * 128)
            yv[b, :, lanes] = jnp.where(lane < 64, halves[0], halves[1]) + rest[:, lanes]

    remote(payload, carry, st_send.at[0], st_recv.at[0], other).wait_recv()
    came = carry[...]
    nothing = jnp.zeros_like(came)
    state = jnp.where(seq == 1, came, nothing)
    for b in range(BLOCKS):
        ef[b] = state.astype(BF16)
        state = decays[b][0] * state + sf[b]
    state = jnp.where(seq == 0, came, nothing)
    for b in reversed(range(BLOCKS)):
        eb[b] = state.astype(BF16)
        state = decays[b][1] * state + sb[b]

    loads[4].wait()
    gain = gain_ref[...]
    ones8 = jnp.ones((8, WIDE), BF16)
    ss1[my_y] = jnp.zeros((8, 128), F32)
    ss2[my_x] = jnp.zeros((8, 128), F32)
    for b in range(BLOCKS):
        rows = slice(b * SPAN, (b + 1) * SPAN)
        inter_f = dot(pfv[1, rows, :], ef[b]) * expc[b, :, :WIDE]
        inter_b = dot(pbv[1, rows, :], eb[b]) * expc[b, :, WIDE:]
        zb = zv[rows, :].astype(F32)
        gated = (yv[b] + inter_f + inter_b) * (zb / (1.0 + jnp.exp(-zb)))
        g = (gated * gain).astype(BF16)
        a1[my_y, b] = g[:HALF]
        a2[my_x, b] = g[HALF:]
        square = split(gated * gated, 2)
        sums = dot_nt(ones8, square[0].astype(BF16)) + dot_nt(ones8, square[1].astype(BF16))
        ss1[my_y, b : b + 1, :] = sums[0:1, :HALF]
        ss2[my_x, b : b + 1, :] = sums[0:1, HALF:]
        if b == BLOCKS - 1:
            for k in range(3):
                start(ss1.at[my_y], ss1.at[my_y], s_send.at[0, k], s_recv.at[0, my_y], to_y[k])
                start(ss2.at[my_x], ss2.at[my_x], s_send.at[1, k], s_recv.at[1, my_x], to_x[k])
        for k in range(3):
            start(a1.at[my_y, b], a1.at[my_y, b], a_send.at[0, k, b], a_recv.at[0, my_y, b], to_y[k])
            start(a2.at[my_x, b], a2.at[my_x, b], a_send.at[1, k, b], a_recv.at[1, my_x, b], to_x[k])

    own_w1.wait()
    own_w2.wait()
    for k in range(3):
        remote(w_hbm.at[:, my_x], w1.at[:, :, tile(xs[k])], w_send.at[0, k], w_recv.at[0, xs[k]], to_x[k]).wait_recv()
        remote(w_hbm.at[my_y], w2.at[:, :, tile(ys[k])], w_send.at[1, k], w_recv.at[1, ys[k]], to_y[k]).wait_recv()
    for b in range(BLOCKS):
        if b == BLOCKS - 1:
            for k in range(3):
                remote(ss1.at[ys[k]], ss1.at[ys[k]], s_send.at[0, k], s_recv.at[0, ys[k]], to_y[k]).wait_recv()
                remote(ss2.at[xs[k]], ss2.at[xs[k]], s_send.at[1, k], s_recv.at[1, xs[k]], to_x[k]).wait_recv()
            so1[my_x] = ss1[0] + ss1[1] + ss1[2] + ss1[3]
            so2[my_y] = ss2[0] + ss2[1] + ss2[2] + ss2[3]
            for k in range(3):
                start(so1.at[my_x], so1.at[my_x], t_send.at[0, k], t_recv.at[0, my_x], to_x[k])
                start(so2.at[my_y], so2.at[my_y], t_send.at[1, k], t_recv.at[1, my_y], to_y[k])
        for plan, (a, w, o, dest, src, peers, back) in enumerate(
            ((a1, w1, os1, or1, ys, xs, to_x), (a2, w2, os2, or2, xs, ys, to_y))
        ):
            mine = my_x if plan == 0 else my_y
            here = to_y if plan == 0 else to_x
            for k in range(3):
                remote(a.at[src[k], b], a.at[src[k], b], a_send.at[plan, k, b], a_recv.at[plan, src[k], b], here[k]).wait_recv()
            lhs = jnp.concatenate([a[j, b] for j in range(SIDE)], axis=1)
            product = dot(lhs, w[...].reshape(SIDE * WIDE, SIDE * COLS)).astype(BF16)
            for j in range(SIDE):
                o[b, j] = product[:, j * COLS : (j + 1) * COLS]
            for k in range(3):
                start(o.at[b, peers[k]], dest.at[mine, b], o_send.at[plan, k, b], o_recv.at[plan, mine, b], back[k])

    for plan, (so, peers, dev) in enumerate(((so1, xs, to_x), (so2, ys, to_y))):
        for k in range(3):
            remote(so.at[peers[k]], so.at[peers[k]], t_send.at[plan, k], t_recv.at[plan, peers[k]], dev[k]).wait_recv()
    scale_parts = []
    for so in (so1, so2):
        scale = lax.rsqrt((so[0] + so[1] + so[2] + so[3]) / INNER + 1.0)
        parts = split(scale, 3) + [jnp.zeros((8, 128), F32)]
        scale_parts.append(jnp.concatenate(parts, axis=0).astype(BF16))
    for b in range(BLOCKS):
        pick_b = jnp.where(((col_row & 7) == b) & (col_row < 24), 1.0, 0.0).astype(BF16)
        for plan, (o, dest, mine, peers, dev) in enumerate(
            ((os1, or1, my_x, xs, to_x), (os2, or2, my_y, ys, to_y))
        ):
            scale = dot_tt(scale_parts[plan], pick_b)
            total = o[b, mine].astype(F32)
            for k in range(3):
                remote(dest.at[peers[k], b], dest.at[peers[k], b], o_send.at[plan, k, b], o_recv.at[plan, peers[k], b], dev[k]).wait_recv()
                total = total + dest[peers[k], b].astype(F32)
            at = b * SPAN + plan * HALF
            out_ref[at : at + HALF, :] = (total * scale).astype(BF16)
    for copy in sends:
        copy.wait_send()


def body(ssm_input, gate_z, proj_forward, proj_backward, step_raw, head_params, skip_gain, norm_gain, out_weight):
    any_spec = pl.BlockSpec(memory_space=pl.ANY)
    smem = pl.BlockSpec(memory_space=pltpu.SMEM)
    vmem = pl.BlockSpec(memory_space=pltpu.VMEM)
    dma = pltpu.SemaphoreType.DMA
    rows = BLOCKS * SPAN
    return pl.pallas_call(
        kernel,
        out_shape=jax.ShapeDtypeStruct((rows, COLS), BF16),
        in_specs=[any_spec] * 5 + [smem, smem, vmem, any_spec],
        out_specs=vmem,
        scratch_shapes=[
            pltpu.VMEM((rows, WIDE), BF16),
            pltpu.VMEM((rows, WIDE), BF16),
            pltpu.VMEM((2, rows, NST), BF16),
            pltpu.VMEM((2, rows, NST), BF16),
            pltpu.VMEM((2, HEADS, rows), F32),
            pltpu.VMEM((SIDE, WIDE, SIDE * COLS), BF16),
            pltpu.VMEM((SIDE, WIDE, SIDE * COLS), BF16),
            pltpu.VMEM((SIDE, BLOCKS, HALF, WIDE), BF16),
            pltpu.VMEM((SIDE, BLOCKS, HALF, WIDE), BF16),
            pltpu.VMEM((BLOCKS, SIDE, HALF, COLS), BF16),
            pltpu.VMEM((BLOCKS, SIDE, HALF, COLS), BF16),
            pltpu.VMEM((SIDE, BLOCKS, HALF, COLS), BF16),
            pltpu.VMEM((SIDE, BLOCKS, HALF, COLS), BF16),
            pltpu.VMEM((SIDE, 8, 128), F32),
            pltpu.VMEM((SIDE, 8, 128), F32),
            pltpu.VMEM((SIDE, 8, 128), F32),
            pltpu.VMEM((SIDE, 8, 128), F32),
            pltpu.VMEM((BLOCKS, SPAN, 2 * WIDE), F32),
            pltpu.VMEM((BLOCKS, SPAN, WIDE), F32),
            pltpu.VMEM((BLOCKS, NST, WIDE), F32),
            pltpu.VMEM((BLOCKS, NST, WIDE), F32),
            pltpu.VMEM((BLOCKS, NST, WIDE), BF16),
            pltpu.VMEM((BLOCKS, NST, WIDE), BF16),
            pltpu.VMEM((NST, WIDE), F32),
            pltpu.VMEM((NST, WIDE), F32),
            dma((7,)),
            dma((2, 3)),
            dma((2, SIDE)),
            dma((1,)),
            dma((1,)),
            dma((2, 3, BLOCKS)),
            dma((2, SIDE, BLOCKS)),
            dma((2, 3)),
            dma((2, SIDE)),
            dma((2, 3, BLOCKS)),
            dma((2, SIDE, BLOCKS)),
            dma((2, 3)),
            dma((2, SIDE)),
        ],
        compiler_params=pltpu.CompilerParams(
            collective_id=0, has_side_effects=True, vmem_limit_bytes=48 * 1024 * 1024
        ),
        name="encoder",
    )(
        ssm_input, gate_z, proj_forward, proj_backward, step_raw, head_params, skip_gain,
        norm_gain.reshape(1, WIDE), out_weight.reshape(SIDE, SIDE, WIDE, COLS),
    )


def solution(mesh):
    in_specs = (
        P(("batch", "seq"), "chan"),
        P(("batch", "seq"), "chan"),
        P(None, ("batch", "seq"), None),
        P(None, ("batch", "seq"), None),
        P(None, "chan", ("batch", "seq")),
        P(None, None, "chan"),
        P("chan"),
        P("chan"),
        P(None, "chan"),
    )
    out_specs = P(("batch", "seq"), "chan")
    return jax.shard_map(body, mesh=mesh, in_specs=in_specs, out_specs=out_specs, check_vma=False)
```

time: 173 us -> 46.1 us (0.27)
  blocking collectives: 47.2 us -> 0 us
  waiting for transfers between devices: 44.4 us -> 0 us
  Pallas kernels: 0 us -> 38.2 us
  matrix products: 20.8 us -> 0 us
  local copies, waits for them, and re-layouts: 26 us -> 7.54 us
  other arithmetic: 18.2 us -> 0 us
  between operations: 14 us -> 0.02 us
    all_to_all x3 -> x0, blocking collectives: 45.3 us -> none  [the longest x1 16.7 us: body(): lax.all_to_all(normed, 'chan', split_axis=0, concat_axis=1, tiled=True)]
    all_gather x1 -> x0, waiting for transfers between devices: 43.7 us -> none  [body(): lax.all_gather(out_weight, 'chan', axis=1, tiled=True)]
    pallas_call x0 -> x1, Pallas kernels: none -> 38.2 us  [body(): pl.pallas_call(kernel, out_shape=jax.ShapeDtypeStruct((rows, COLS), BF16)...]
    dot_general x9 -> x0, matrix products: 20.8 us -> none  [the longest x1 8.79 us: body(): jnp.dot(frame_share, lax.all_gather(out_weight, 'chan', axis=1, tiled=Tru...]
    rev x5 -> x0, local copies, waits for them, and re-layouts: 12 us -> none  [the longest x1 6.33 us: body(): ssm_input[::-1].reshape(shape_x)]
    another operation x13 -> x0, other arithmetic: 9.99 us -> none
    unnamed x47 -> x19, local copies, waits for them, and re-layouts: 4.97 us -> 7.54 us
    reduce_sum x4 -> x0, other arithmetic: 2.26 us -> none  [the longest x1 1.83 us: body(): squares = taken_together(jnp.sum(gated * gated, axis=1), 'chan')]
  transfers between devices with their start and end apart: 1 -> 0, of which waited for: 1 -> 0; matrix products, arithmetic and copies ran while one was open for 32% -> 0% of each run, Pallas kernels for 0% -> 0%
where the time goes in v1:
time: 46.1 us; the launch traced here: 45.7 us
  Pallas kernels  38.2 us (83%)
  local copies, waits for them, and re-layouts  7.54 us (16%)
    pallas_call x1, Pallas kernels, body(): pl.pallas_call(kernel, out_shape=jax.ShapeDtypeStruct((rows, COLS), BF16)...  38.2 us
    unnamed x19, local copies, waits for them, and re-layouts  7.54 us

profile of v1, /device:TPU:32, one launch (start us, length us, event | category | flops | bytes accessed | tf_op | source)
XLA Modules:
  0.0 45.7 jit_solution(11010685539140961445)
XLA Ops:
  0.0 0.0 copy-start.6
  0.0 0.0 copy-start.7
  0.0 0.0 copy-start.8
  0.0 0.7 %copy-done.6 = f32[2,2,4]{2,1,0:T(2,128)S(1)} copy-done((f32[2,2,4]{2,1,0:T(2,128)S(1)}, f32[2,2,4]{2,1,0:T(2,128)}, u32[]{:S(2)}) %copy-start.6) | copy-done | bytes 88
  0.7 0.0 copy-done.7
  0.7 0.0 copy-done.8
  0.7 0.0 copy-start
  0.7 1.2 %copy-done = bf16[4096,128]{1,0:T(8,128)(2,1)S(1)} copy-done((bf16[4096,128]{1,0:T(8,128)(2,1)S(1)}, bf16[4096,128]{1,0:T(8,128)(2,1)}, u32[]{:S(2)}) %copy-start) | copy-done | bytes 1048600
  1.9 0.0 copy-start.1
  1.9 1.0 %copy-done.1 = bf16[1024,256]{1,0:T(8,128)(2,1)S(1)} copy-done((bf16[1024,256]{1,0:T(8,128)(2,1)S(1)}, bf16[1024,256]{1,0:T(8,128)(2,1)}, u32[]{:S(2)}) %copy-start.1) | copy-done | bytes 524312
  3.0 0.0 copy-start.2
  3.0 1.0 %copy-done.2 = bf16[1024,256]{1,0:T(8,128)(2,1)S(1)} copy-done((bf16[1024,256]{1,0:T(8,128)(2,1)S(1)}, bf16[1024,256]{1,0:T(8,128)(2,1)}, u32[]{:S(2)}) %copy-start.2) | copy-done | bytes 524312
  4.0 0.0 copy-start.3
  4.0 1.0 %copy-done.3 = bf16[2,1024,128]{2,1,0:T(8,128)(2,1)S(1)} copy-done((bf16[2,1024,128]{2,1,0:T(8,128)(2,1)S(1)}, bf16[2,1024,128]{2,1,0:T(8,128)(2,1)}, u32[]{:S(2)}) %copy-start.3) | copy-done | bytes 524312
  5.1 0.0 copy-start.4
  5.1 1.0 %copy-done.4 = bf16[2,1024,128]{2,1,0:T(8,128)(2,1)S(1)} copy-done((bf16[2,1024,128]{2,1,0:T(8,128)(2,1)S(1)}, bf16[2,1024,128]{2,1,0:T(8,128)(2,1)}, u32[]{:S(2)}) %copy-start.4) | copy-done | bytes 524312
  6.1 0.0 copy-start.5
  6.1 0.8 %copy-done.5 = f32[2,4,1024]{2,1,0:T(4,128)S(1)} copy-done((f32[2,4,1024]{2,1,0:T(4,128)S(1)}, f32[2,4,1024]{2,1,0:T(4,128)}, u32[]{:S(2)}) %copy-start.5) | copy-done | bytes 32792
  6.9 38.2 %encoder.1 = bf16[1024,128]{1,0:T(8,128)(2,1)S(1)} custom-call(bf16[1024,256]{1,0:T(8,128)(2,1)S(1)} %copy-done.1, bf16[1024,256]{1,0:T(8,128)(2,1)S(1)} %copy-done.2, bf16[2,1024,128]{2,1,0:T(8,128)(2,1)S(1)} %copy-done.3, bf16[2,1024,128]{2,1,0:T(8,128)(2,1)S(1)} %copy-done.4, f32[2,4,1024]{2,1,0:T(4,128)S(1)} %copy-done.5, f32[2,2,4]{2,1,0:T(2,128)S(1)} %copy-done.6, ...), custom_call_target="tpu_custom_call" | custom-call | tf_op jit(solution)/shard_map/encoder/pallas_call | solution.py:285
  45.0 0.7 %copy.11 = bf16[1024,128]{1,0:T(8,128)(2,1)} copy(bf16[1024,128]{1,0:T(8,128)(2,1)S(1)} %encoder.1) | data formatting | bytes 524288
Async XLA Ops:
  0.0 0.7 %copy-start.6 = (f32[2,2,4]{2,1,0:T(2,128)S(1)}, f32[2,2,4]{2,1,0:T(2,128)}, u32[]{:S(2)}) copy-start(f32[2,2,4]{2,1,0:T(2,128)} %hp.1) | copy-start | bytes 196
  0.0 0.7 %copy-start.7 = (f32[256]{0:T(256)S(1)}, f32[256]{0:T(256)}, u32[]{:S(2)}) copy-start(f32[256]{0:T(256)} %param.16) | copy-start | bytes 3076
  0.0 0.7 %copy-start.8 = (f32[4]{0:T(128)S(1)}, f32[4]{0:T(128)}, u32[]{:S(2)}) copy-start(f32[4]{0:T(128)} %skip.1) | copy-start | bytes 52
  0.7 1.2 %copy-start = (bf16[4096,128]{1,0:T(8,128)(2,1)S(1)}, bf16[4096,128]{1,0:T(8,128)(2,1)}, u32[]{:S(2)}) copy-start(bf16[4096,128]{1,0:T(8,128)(2,1)} %param.17) | copy-start | bytes 3145732
  1.9 1.0 %copy-start.1 = (bf16[1024,256]{1,0:T(8,128)(2,1)S(1)}, bf16[1024,256]{1,0:T(8,128)(2,1)}, u32[]{:S(2)}) copy-start(bf16[1024,256]{1,0:T(8,128)(2,1)} %x_hbm.1) | copy-start | bytes 1572868
  3.0 1.0 %copy-start.2 = (bf16[1024,256]{1,0:T(8,128)(2,1)S(1)}, bf16[1024,256]{1,0:T(8,128)(2,1)}, u32[]{:S(2)}) copy-start(bf16[1024,256]{1,0:T(8,128)(2,1)} %z_hbm.1) | copy-start | bytes 1572868
  4.0 1.0 %copy-start.3 = (bf16[2,1024,128]{2,1,0:T(8,128)(2,1)S(1)}, bf16[2,1024,128]{2,1,0:T(8,128)(2,1)}, u32[]{:S(2)}) copy-start(bf16[2,1024,128]{2,1,0:T(8,128)(2,1)} %pf_hbm.1) | copy-start | bytes 1572868
  5.1 1.0 %copy-start.4 = (bf16[2,1024,128]{2,1,0:T(8,128)(2,1)S(1)}, bf16[2,1024,128]{2,1,0:T(8,128)(2,1)}, u32[]{:S(2)}) copy-start(bf16[2,1024,128]{2,1,0:T(8,128)(2,1)} %pb_hbm.1) | copy-start | bytes 1572868
  6.1 0.8 %copy-start.5 = (f32[2,4,1024]{2,1,0:T(4,128)S(1)}, f32[2,4,1024]{2,1,0:T(4,128)}, u32[]{:S(2)}) copy-start(f32[2,4,1024]{2,1,0:T(4,128)} %st_hbm.1) | copy-start | bytes 98308

commit v2 on v1

v2 whole, which is shorter than its diff:
```python
import jax
import jax.numpy as jnp
from jax import lax
from jax.experimental import pallas as pl
from jax.experimental.pallas import tpu as pltpu
from jax.sharding import PartitionSpec as P

MESH = pl.DeviceIdType.MESH


class Phases:
    def __init__(self):
        self.now = None

    def __call__(self, name):
        if self.now is not None:
            self.now.__exit__(None, None, None)
        self.now = None
        if name is not None:
            self.now = jax.named_scope(name)
            self.now.__enter__()


F32, BF16 = jnp.float32, jnp.bfloat16
SPAN = 256
HALF = 128
BLOCKS = 4
HEADS = 4
WIDE = 256
SIDE = 4
COLS = 128
NST = 128
INNER = 4096
LOG2E = 1.4426950408889634


def iota(shape, dim):
    return lax.broadcasted_iota(jnp.int32, shape, dim)


def dot(a, b):
    return jnp.dot(a, b, preferred_element_type=F32)


def dot_tt(a, b):
    return lax.dot_general(a, b, (((0,), (0,)), ((), ())), preferred_element_type=F32)


def dot_nt(a, b):
    return lax.dot_general(a, b, (((1,), (1,)), ((), ())), preferred_element_type=F32)


def split(v, parts):
    out = []
    for _ in range(parts - 1):
        high = v.astype(BF16).astype(F32)
        out.append(high)
        v = v - high
    out.append(v)
    return out


def tile(i):
    return pl.ds(pl.multiple_of(i * COLS, COLS), COLS)


def kernel(
    x_hbm, z_hbm, pf_hbm, pb_hbm, st_hbm, hp_hbm, skip_hbm, gain_hbm, w_hbm, out_ref,
    hp, skip, gain_ref, xv, zv, pfv, pbv, stv, w1, w2, a1, a2, os1, os2, or1, or2,
    ss1, ss2, so1, so2, yv, sf, sb, ef, eb, payload, carry, ov,
    in_sem, w_send, w_recv, v_send, v_recv, st_send, st_recv,
    a_send, a_recv, r_recv, s_send, s_recv, t_send, t_recv, o_send, o_recv, out_sem,
):
    seq, chan = lax.axis_index("seq"), lax.axis_index("chan")
    my_y, my_x = chan // SIDE, lax.rem(chan, SIDE)
    phase = Phases()

    phase("entry")
    loads = []
    for i, (src, dst) in enumerate(
        (
            (hp_hbm, hp), (st_hbm, stv), (x_hbm, xv), (pf_hbm, pfv), (pb_hbm, pbv),
            (z_hbm, zv), (skip_hbm, skip), (gain_hbm, gain_ref),
            (w_hbm.at[:, my_x], w1.at[:, :, tile(my_x)]), (w_hbm.at[my_y], w2.at[:, :, tile(my_y)]),
        )
    ):
        copy = pltpu.make_async_copy(src, dst, in_sem.at[i])
        copy.start()
        loads.append(copy)

    ys = [lax.rem(my_y + k, SIDE) for k in range(1, SIDE)]
    xs = [lax.rem(my_x + k, SIDE) for k in range(1, SIDE)]
    to_y = [{"chan": v * SIDE + my_x} for v in ys]
    to_x = [{"chan": my_y * SIDE + v} for v in xs]
    other = {"seq": 1 - seq}
    barrier = pltpu.get_barrier_semaphore()
    for dev in to_y + to_x + [other]:
        pl.semaphore_signal(barrier, inc=1, device_id=dev, device_id_type=MESH)
    pl.semaphore_wait(barrier, 7)

    def remote(src, dst, send, recv, dev):
        return pltpu.make_async_remote_copy(
            src_ref=src, dst_ref=dst, send_sem=send, recv_sem=recv,
            device_id=dev, device_id_type=MESH,
        )

    def start(*args):
        remote(*args).start()

    def arrived(ref, send, recv, dev):
        remote(ref, ref, send, recv, dev).wait_recv()

    plans = (
        (a1, w1, os1, or1, ss1, so1, my_y, ys, to_y, my_x, xs, to_x),
        (a2, w2, os2, or2, ss2, so2, my_x, xs, to_x, my_y, ys, to_y),
    )

    half = pl.ds(2 * seq, 2)
    for k in range(3):
        start(w_hbm.at[half, xs[k]], w1.at[half, :, tile(my_x)], w_send.at[0], w_recv.at[0], to_x[k])
        start(w_hbm.at[ys[k], half], w2.at[half, :, tile(my_y)], w_send.at[1], w_recv.at[1], to_y[k])

    def three(w):
        return w.at[pl.ds(0, 2), :, pl.ds(0, 3 * COLS)]

    def pass_weights_on():
        phase("weights1")
        for p, plan in enumerate(plans):
            w, peers, dev = plan[1], plan[10], plan[11]
            arrived(three(w), w_send.at[p], w_recv.at[p], dev[0])
            for k in range(3):
                piece = w.at[half, :, tile(peers[k])]
                start(piece, piece, v_send.at[p], v_recv.at[p], other)

    def all_weights():
        phase("weights2")
        loads[8].wait()
        loads[9].wait()
        for p, plan in enumerate(plans):
            arrived(three(plan[1]), v_send.at[p], v_recv.at[p], other)

    phase("steps")
    loads[0].wait()
    loads[1].wait()
    row8 = iota((8, BLOCKS * SPAN), 0)
    bias = jnp.zeros((8, BLOCKS * SPAN), F32)
    rate = jnp.zeros((8, BLOCKS * SPAN), F32)
    for j in range(8):
        bias = jnp.where(row8 == j, hp[j // 4, 1, j % 4], bias)
        rate = jnp.where(row8 == j, hp[j // 4, 0, j % 4], rate)
    raw = jnp.concatenate([stv[0], stv[1]], axis=0) + bias
    dt_all = jnp.maximum(raw, 0.0) + jnp.log1p(jnp.exp(-jnp.abs(raw)))
    logs = split(-rate * dt_all, 3)
    stacked = jnp.concatenate(
        [part[:, b * SPAN : (b + 1) * SPAN] for b in range(BLOCKS) for part in logs], axis=0
    ).astype(BF16)
    t_of, s_of = iota((SPAN, SPAN), 0), iota((SPAN, SPAN), 1)
    after = t_of >= s_of
    up_to = dot(stacked, jnp.where(t_of <= s_of, 1.0, 0.0).astype(BF16))
    down_to = dot(stacked, jnp.where(after, 1.0, 0.0).astype(BF16))
    is_fwd = iota((8, SPAN), 0) < HEADS
    spread_row, spread_col = iota((16, 2 * WIDE), 0), iota((16, 2 * WIDE), 1)
    spread = jnp.where((spread_row & 7) == (spread_col >> 6), 1.0, 0.0).astype(BF16)
    pick_row, pick_col = iota((32, 128), 0), iota((32, 128), 1)

    def pick(which):
        return jnp.where(((pick_row & 7) == which) & (pick_row < 24), 1.0, 0.0).astype(BF16)

    pick_own = pick(pick_col)
    zero8 = jnp.zeros((8, SPAN), F32)
    chan_row = iota((1, WIDE), 1) >> 6

    def by_head(values):
        row = jnp.zeros((1, WIDE), F32)
        for h in range(HEADS):
            row = jnp.where(chan_row == h, values[h], row)
        return row

    phase("block_states")
    cum2, cprime, dts, decays, grows = [], [], [], [], []
    for copy in loads[2:5]:
        copy.wait()
    for b in range(BLOCKS):
        at, rows = b * 24, slice(b * SPAN, (b + 1) * SPAN)
        c_f = up_to[at : at + 8] + up_to[at + 8 : at + 16] + up_to[at + 16 : at + 24]
        c_b = down_to[at : at + 8] + down_to[at + 8 : at + 16] + down_to[at + 16 : at + 24]
        cum = jnp.where(is_fwd, c_f, c_b)
        end = jnp.where(is_fwd, cum[:, SPAN - 1 : SPAN], cum[:, 0:1])
        dt = dt_all[:, rows]
        e = jnp.exp(cum)
        w = jnp.exp(end - cum) * dt
        c2 = cum * LOG2E
        cum2.append(c2)
        cprime.append(c2 - jnp.log2(dt))
        dts.append(dt)
        grows.append(e)
        decays.append(
            (
                by_head([e[h : h + 1, SPAN - 1 : SPAN] for h in range(HEADS)]),
                by_head([e[HEADS + h : HEADS + h + 1, 0:1] for h in range(HEADS)]),
            )
        )
        w_cols = dot_tt(jnp.concatenate(split(w, 2), axis=0).astype(BF16), spread)
        xb = xv[rows, :].astype(F32)
        sf[b] = dot_tt(pfv[0, rows, :], (xb * w_cols[:, :WIDE]).astype(BF16))
        sb[b] = dot_tt(pbv[0, rows, :], (xb * w_cols[:, WIDE:]).astype(BF16))

    end_f = sf[0]
    for b in range(1, BLOCKS):
        end_f = decays[b][0] * end_f + sf[b]
    end_b = sb[BLOCKS - 1]
    for b in reversed(range(BLOCKS - 1)):
        end_b = decays[b][1] * end_b + sb[b]
    payload[...] = jnp.where(seq == 0, end_f, end_b)
    start(payload, carry, st_send.at[0], st_recv.at[0], other)

    loads[6].wait()
    skip_row = by_head([skip[h] for h in range(HEADS)])
    lane = iota((SPAN, 128), 1)

    def intra(b):
        phase(f"intra{b}")
        rows = slice(b * SPAN, (b + 1) * SPAN)
        b_f, c_f = pfv[0, rows, :], pfv[1, rows, :]
        b_b, c_b = pbv[0, rows, :], pbv[1, rows, :]
        scores = jnp.where(after, dot_nt(c_f, b_f), dot_nt(c_b, b_b))
        cols = dot_tt(jnp.concatenate(split(cum2[b], 3) + [zero8], axis=0).astype(BF16), pick_own)
        dt_cols = dot_tt(jnp.concatenate(split(dts[b], 2), axis=0).astype(BF16), spread[:, WIDE:])
        xb = xv[rows, :]
        same = jnp.sum(c_b.astype(F32) * b_b.astype(F32), axis=1, keepdims=True)
        rest = xb.astype(F32) * (same * dt_cols + skip_row)
        for pair in range(2):
            halves = []
            for h in (2 * pair, 2 * pair + 1):
                gaps = jnp.where(
                    after,
                    cols[:, h : h + 1] - cprime[b][h : h + 1, :],
                    cols[:, 4 + h : 5 + h] - cprime[b][4 + h : 5 + h, :],
                )
                weights = (scores * jnp.exp2(gaps)).astype(BF16)
                halves.append(dot(weights, xb[:, pair * 128 : (pair + 1) * 128]))
            lanes = slice(pair * 128, (pair + 1) * 128)
            yv[b, :, lanes] = jnp.where(lane < 64, halves[0], halves[1]) + rest[:, lanes]

    def enter():
        phase("carry")
        arrived(carry, st_send.at[0], st_recv.at[0], other)
        came = carry[...]
        nothing = jnp.zeros_like(came)
        state = jnp.where(seq == 1, came, nothing)
        for b in range(BLOCKS):
            ef[b] = state.astype(BF16)
            state = decays[b][0] * state + sf[b]
        state = jnp.where(seq == 0, came, nothing)
        for b in reversed(range(BLOCKS)):
            eb[b] = state.astype(BF16)
            state = decays[b][1] * state + sb[b]
        loads[5].wait()
        loads[7].wait()
        ss1[my_y] = jnp.zeros((8, 128), F32)
        ss2[my_x] = jnp.zeros((8, 128), F32)

    ones8 = jnp.ones((8, WIDE), BF16)

    def gate(b):
        phase(f"gate{b}")
        rows = slice(b * SPAN, (b + 1) * SPAN)
        e_cols = dot_tt(jnp.concatenate(split(grows[b], 2), axis=0).astype(BF16), spread)
        inter_f = dot(pfv[1, rows, :], ef[b]) * e_cols[:, :WIDE]
        inter_b = dot(pbv[1, rows, :], eb[b]) * e_cols[:, WIDE:]
        zb = zv[rows, :].astype(F32)
        gated = (yv[b] + inter_f + inter_b) * (zb / (1.0 + jnp.exp(-zb)))
        g = (gated * gain_ref[...]).astype(BF16)
        a1[my_y, b] = g[:HALF]
        a2[my_x, b] = g[HALF:]
        square = split(gated * gated, 2)
        sums = dot_nt(ones8, square[0].astype(BF16)) + dot_nt(ones8, square[1].astype(BF16))
        ss1[my_y, b : b + 1, :] = sums[0:1, :HALF]
        ss2[my_x, b : b + 1, :] = sums[0:1, HALF:]
        for k in (0, 2, 1):
            for p, plan in enumerate(plans):
                a, ss, mine, dev = plan[0], plan[4], plan[6], plan[8]
                if b == BLOCKS - 1:
                    start(ss.at[mine], ss.at[mine], s_send.at[p], s_recv.at[p], dev[k])
                if b == BLOCKS - 1 or k != 1:
                    start(a.at[mine, b], a.at[mine, b], a_send.at[p], a_recv.at[p, b], dev[k])

    def relay(b):
        phase(f"relay{b}")
        for p, plan in enumerate(plans):
            a, src, dev = plan[0], plan[7], plan[8]
            arrived(a.at[pl.ds(0, 2), b], a_send.at[p], a_recv.at[p, b], dev[0])
            for i, k in enumerate((2, 0)):
                half = a.at[src[k], b, pl.ds(i * 64, 64)]
                start(half, half, a_send.at[p], r_recv.at[p, b], dev[2 - k])

    def product(b):
        for p, (a, w, o, dest, ss, so, _, _, dev, mine, peers, back) in enumerate(plans):
            phase(f"wait{b}{p}")
            if b < BLOCKS - 1:
                arrived(a.at[0, b], a_send.at[p], r_recv.at[p, b], dev[0])
            else:
                arrived(a.at[pl.ds(0, 3), b], a_send.at[p], a_recv.at[p, b], dev[0])
            phase(f"product{b}{p}")
            lhs = jnp.concatenate([a[j, b] for j in range(SIDE)], axis=1)
            values = dot(lhs, w[...].reshape(SIDE * WIDE, SIDE * COLS)).astype(BF16)
            for j in range(SIDE):
                o[b, j] = values[:, j * COLS : (j + 1) * COLS]
            for k in range(3):
                start(o.at[b, peers[k]], dest.at[mine, b], o_send.at[p], o_recv.at[p, b], back[k])

    def squares():
        phase("squares")
        for p, (_, _, _, _, ss, so, _, _, dev, mine, _, back) in enumerate(plans):
            arrived(ss.at[pl.ds(0, 3)], s_send.at[p], s_recv.at[p], dev[0])
            so[mine] = ss[0] + ss[1] + ss[2] + ss[3]
            for k in range(3):
                start(so.at[mine], so.at[mine], t_send.at[p], t_recv.at[p], back[k])

    intra(0)
    enter()
    gate(0)
    intra(1)
    gate(1)
    intra(2)
    gate(2)
    pass_weights_on()
    intra(3)
    gate(3)
    relay(0)
    relay(1)
    all_weights()
    relay(2)
    product(0)
    product(1)
    squares()
    product(2)
    product(3)

    phase("scale")
    scales = []
    for p, plan in enumerate(plans):
        so, back = plan[5], plan[11]
        arrived(so.at[pl.ds(0, 3)], t_send.at[p], t_recv.at[p], back[0])
        scale = lax.rsqrt((so[0] + so[1] + so[2] + so[3]) / INNER + 1.0)
        parts = split(scale, 3) + [jnp.zeros((8, 128), F32)]
        scales.append(jnp.concatenate(parts, axis=0).astype(BF16))
    for b in range(BLOCKS):
        phase(f"out{b}")
        pick_b = pick(b)
        for p, (_, _, o, dest, _, _, _, _, _, mine, peers, back) in enumerate(plans):
            scale = dot_tt(scales[p], pick_b)
            arrived(dest.at[pl.ds(0, 3), b], o_send.at[p], o_recv.at[p, b], back[0])
            total = o[b, mine].astype(F32)
            for k in range(3):
                total = total + dest[peers[k], b].astype(F32)
            at = b * SPAN + p * HALF
            ov[at : at + HALF, :] = (total * scale).astype(BF16)
        rows = pl.ds(b * SPAN, SPAN)
        pltpu.make_async_copy(ov.at[rows], out_ref.at[rows], out_sem.at[0]).start()

    phase("drain")
    pltpu.make_async_copy(ov, out_ref, out_sem.at[0]).wait()
    remote(payload, carry, st_send.at[0], st_recv.at[0], other).wait_send()
    for p, (a, w, o, dest, ss, so, _, _, dev, _, _, back) in enumerate(plans):
        for ref, send, recv in (
            (three(w), w_send.at[p], w_recv.at[p]),
            (three(w), v_send.at[p], v_recv.at[p]),
            (a.at[pl.ds(0, 3)], a_send.at[p], a_recv.at[p, 0]),
            (ss.at[pl.ds(0, 3)], s_send.at[p], s_recv.at[p]),
            (so.at[pl.ds(0, 3)], t_send.at[p], t_recv.at[p]),
            (o.at[:, pl.ds(0, 3)], o_send.at[p], o_recv.at[p, 0]),
        ):
            remote(ref, ref, send, recv, dev[0]).wait_send()
    phase(None)


def body(ssm_input, gate_z, proj_forward, proj_backward, step_raw, head_params, skip_gain, norm_gain, out_weight):
    hbm = pl.BlockSpec(memory_space=pltpu.HBM)
    dma = pltpu.SemaphoreType.DMA
    rows = BLOCKS * SPAN
    return pl.pallas_call(
        kernel,
        out_shape=jax.ShapeDtypeStruct((rows, COLS), BF16),
        in_specs=[hbm] * 9,
        out_specs=pl.BlockSpec(memory_space=pl.ANY),
        scratch_shapes=[
            pltpu.SMEM((2, 2, HEADS), F32),
            pltpu.SMEM((HEADS,), F32),
            pltpu.VMEM((1, WIDE), F32),
            pltpu.VMEM((rows, WIDE), BF16),
            pltpu.VMEM((rows, WIDE), BF16),
            pltpu.VMEM((2, rows, NST), BF16),
            pltpu.VMEM((2, rows, NST), BF16),
            pltpu.VMEM((2, HEADS, rows), F32),
            *[pltpu.VMEM((SIDE, WIDE, SIDE * COLS), BF16)] * 2,
            *[pltpu.VMEM((SIDE, BLOCKS, HALF, WIDE), BF16)] * 2,
            *[pltpu.VMEM((BLOCKS, SIDE, HALF, COLS), BF16)] * 2,
            *[pltpu.VMEM((SIDE, BLOCKS, HALF, COLS), BF16)] * 2,
            *[pltpu.VMEM((SIDE, 8, 128), F32)] * 4,
            pltpu.VMEM((BLOCKS, SPAN, WIDE), F32),
            *[pltpu.VMEM((BLOCKS, NST, WIDE), F32)] * 2,
            *[pltpu.VMEM((BLOCKS, NST, WIDE), BF16)] * 2,
            *[pltpu.VMEM((NST, WIDE), F32)] * 2,
            pltpu.VMEM((rows, COLS), BF16),
            dma((10,)),
            *[dma((2,))] * 4,
            *[dma((1,))] * 2,
            dma((2,)),
            dma((2, BLOCKS)),
            dma((2, BLOCKS - 1)),
            *[dma((2,))] * 5,
            dma((2, BLOCKS)),
            dma((1,)),
        ],
        compiler_params=pltpu.CompilerParams(
            collective_id=0, has_side_effects=True, vmem_limit_bytes=48 * 1024 * 1024
        ),
        name="encoder",
    )(*[
        pltpu.with_memory_space_constraint(v, pltpu.HBM)
        for v in (
            ssm_input, gate_z, proj_forward, proj_backward, step_raw, head_params, skip_gain,
            norm_gain.reshape(1, WIDE), out_weight.reshape(SIDE, SIDE, WIDE, COLS),
        )
    ])


def solution(mesh):
    in_specs = (
        P(("batch", "seq"), "chan"),
        P(("batch", "seq"), "chan"),
        P(None, ("batch", "seq"), None),
        P(None, ("batch", "seq"), None),
        P(None, "chan", ("batch", "seq")),
        P(None, None, "chan"),
        P("chan"),
        P("chan"),
        P(None, "chan"),
    )
    out_specs = P(("batch", "seq"), "chan")
    return jax.shard_map(body, mesh=mesh, in_specs=in_specs, out_specs=out_specs, check_vma=False)
```

time: 46.1 us -> 29.5 us (0.64)
  Pallas kernels: 38.2 us -> 28.7 us
  local copies, waits for them, and re-layouts: 7.54 us -> 0.71 us
    pallas_call x1, Pallas kernels: 38.2 us -> 28.7 us  [body(): pl.pallas_call(kernel, out_shape=jax.ShapeDtypeStruct((rows, COLS), BF16)...]
    unnamed x19 -> x1, local copies, waits for them, and re-layouts: 7.54 us -> 0.71 us
where the time goes in v2:
time: 29.5 us; the launch traced here: 29.4 us
  Pallas kernels  28.7 us (97%)
  local copies, waits for them, and re-layouts  0.71 us (2%)
    pallas_call x1, Pallas kernels, body(): pl.pallas_call(kernel, out_shape=jax.ShapeDtypeStruct((rows, COLS), BF16)...  28.7 us
    unnamed x1, local copies, waits for them, and re-layouts  0.71 us

profile of v2, /device:TPU:32, one launch (start us, length us, event | category | flops | bytes accessed | tf_op | source)
XLA Modules:
  0.0 29.4 jit_solution(14102689257975210076)
XLA Ops:
  0.0 28.7 %encoder.1 = bf16[1024,128]{1,0:T(8,128)(2,1)S(1)} custom-call(bf16[1024,256]{1,0:T(8,128)(2,1)} %x_hbm.1, bf16[1024,256]{1,0:T(8,128)(2,1)} %z_hbm.1, bf16[2,1024,128]{2,1,0:T(8,128)(2,1)} %pf_hbm.1, bf16[2,1024,128]{2,1,0:T(8,128)(2,1)} %pb_hbm.1, f32[2,4,1024]{2,1,0:T(4,128)} %st_hbm.1, f32[2,2,4]{2,1,0:T(2,128)} %hp_hbm.1, f32[4]{0:T(128)} %skip_hbm.1, ...), custom_call_target="tpu_custom_call" | custom-call | tf_op jit(solution)/shard_map/encoder/pallas_call | solution.py:382
  28.7 0.7 %copy.11 = bf16[1024,128]{1,0:T(8,128)(2,1)} copy(bf16[1024,128]{1,0:T(8,128)(2,1)S(1)} %encoder.1) | data formatting | bytes 524288

commit v3 on v2

--- a/solution.py
+++ b/solution.py
@@ -29,6 +29,7 @@
 WIDE = 256
 SIDE = 4
 COLS = 128
+RELAYED = (0, 1, 2)
 NST = 128
 INNER = 4096
 LOG2E = 1.4426950408889634
@@ -66,28 +67,16 @@
 
 def kernel(
     x_hbm, z_hbm, pf_hbm, pb_hbm, st_hbm, hp_hbm, skip_hbm, gain_hbm, w_hbm, out_ref,
-    hp, skip, gain_ref, xv, zv, pfv, pbv, stv, w1, w2, a1, a2, os1, os2, or1, or2,
-    ss1, ss2, so1, so2, yv, sf, sb, ef, eb, payload, carry, ov,
+    wv, hp, skip, gain_ref, xv, zv, pfv, pbv, stv, w1, w2, a1, a2, os1, os2, or1, or2,
+    ss1, ss2, so1, so2, yv, sf, sb, ef, eb, payload, carry,
     in_sem, w_send, w_recv, v_send, v_recv, st_send, st_recv,
-    a_send, a_recv, r_recv, s_send, s_recv, t_send, t_recv, o_send, o_recv, out_sem,
+    a_send, a_recv, r_recv, s_send, s_recv, t_send, t_recv, o_send, o_recv,
 ):
     seq, chan = lax.axis_index("seq"), lax.axis_index("chan")
     my_y, my_x = chan // SIDE, lax.rem(chan, SIDE)
     phase = Phases()
 
     phase("entry")
-    loads = []
-    for i, (src, dst) in enumerate(
-        (
-            (hp_hbm, hp), (st_hbm, stv), (x_hbm, xv), (pf_hbm, pfv), (pb_hbm, pbv),
-            (z_hbm, zv), (skip_hbm, skip), (gain_hbm, gain_ref),
-            (w_hbm.at[:, my_x], w1.at[:, :, tile(my_x)]), (w_hbm.at[my_y], w2.at[:, :, tile(my_y)]),
-        )
-    ):
-        copy = pltpu.make_async_copy(src, dst, in_sem.at[i])
-        copy.start()
-        loads.append(copy)
-
     ys = [lax.rem(my_y + k, SIDE) for k in range(1, SIDE)]
     xs = [lax.rem(my_x + k, SIDE) for k in range(1, SIDE)]
     to_y = [{"chan": v * SIDE + my_x} for v in ys]
@@ -96,7 +85,19 @@
     barrier = pltpu.get_barrier_semaphore()
     for dev in to_y + to_x + [other]:
         pl.semaphore_signal(barrier, inc=1, device_id=dev, device_id_type=MESH)
+    loads = []
+    for i, (src, dst) in enumerate(
+        (
+            (w_hbm, wv), (hp_hbm, hp), (st_hbm, stv), (x_hbm, xv), (pf_hbm, pfv), (pb_hbm, pbv),
+            (z_hbm, zv), (skip_hbm, skip), (gain_hbm, gain_ref),
+            (w_hbm.at[:, my_x], w1.at[:, :, tile(my_x)]), (w_hbm.at[my_y], w2.at[:, :, tile(my_y)]),
+        )
+    ):
+        copy = pltpu.make_async_copy(src, dst, in_sem.at[i])
+        copy.start()
+        loads.append(copy)
     pl.semaphore_wait(barrier, 7)
+    loads[0].wait()
 
     def remote(src, dst, send, recv, dev):
         return pltpu.make_async_remote_copy(
@@ -117,8 +118,8 @@
 
     half = pl.ds(2 * seq, 2)
     for k in range(3):
-        start(w_hbm.at[half, xs[k]], w1.at[half, :, tile(my_x)], w_send.at[0], w_recv.at[0], to_x[k])
-        start(w_hbm.at[ys[k], half], w2.at[half, :, tile(my_y)], w_send.at[1], w_recv.at[1], to_y[k])
+        start(wv.at[half, xs[k]], w1.at[half, :, tile(my_x)], w_send.at[0], w_recv.at[0], to_x[k])
+        start(wv.at[ys[k], half], w2.at[half, :, tile(my_y)], w_send.at[1], w_recv.at[1], to_y[k])
 
     def three(w):
         return w.at[pl.ds(0, 2), :, pl.ds(0, 3 * COLS)]
@@ -134,14 +135,14 @@
 
     def all_weights():
         phase("weights2")
-        loads[8].wait()
         loads[9].wait()
+        loads[10].wait()
         for p, plan in enumerate(plans):
             arrived(three(plan[1]), v_send.at[p], v_recv.at[p], other)
 
     phase("steps")
-    loads[0].wait()
     loads[1].wait()
+    loads[2].wait()
     row8 = iota((8, BLOCKS * SPAN), 0)
     bias = jnp.zeros((8, BLOCKS * SPAN), F32)
     rate = jnp.zeros((8, BLOCKS * SPAN), F32)
@@ -178,7 +179,7 @@
 
     phase("block_states")
     cum2, cprime, dts, decays, grows = [], [], [], [], []
-    for copy in loads[2:5]:
+    for copy in loads[3:6]:
         copy.wait()
     for b in range(BLOCKS):
         at, rows = b * 24, slice(b * SPAN, (b + 1) * SPAN)
@@ -214,7 +215,7 @@
     payload[...] = jnp.where(seq == 0, end_f, end_b)
     start(payload, carry, st_send.at[0], st_recv.at[0], other)
 
-    loads[6].wait()
+    loads[7].wait()
     skip_row = by_head([skip[h] for h in range(HEADS)])
     lane = iota((SPAN, 128), 1)
 
@@ -255,8 +256,8 @@
         for b in reversed(range(BLOCKS)):
             eb[b] = state.astype(BF16)
             state = decays[b][1] * state + sb[b]
-        loads[5].wait()
-        loads[7].wait()
+        loads[6].wait()
+        loads[8].wait()
         ss1[my_y] = jnp.zeros((8, 128), F32)
         ss2[my_x] = jnp.zeros((8, 128), F32)
 
@@ -277,13 +278,21 @@
         sums = dot_nt(ones8, square[0].astype(BF16)) + dot_nt(ones8, square[1].astype(BF16))
         ss1[my_y, b : b + 1, :] = sums[0:1, :HALF]
         ss2[my_x, b : b + 1, :] = sums[0:1, HALF:]
-        for k in (0, 2, 1):
+        if b == BLOCKS - 1:
+            for k in range(3):
+                for p, plan in enumerate(plans):
+                    ss, mine, dev = plan[4], plan[6], plan[8]
+                    start(ss.at[mine], ss.at[mine], s_send.at[p], s_recv.at[p], dev[k])
+        for k in (0, 2):
             for p, plan in enumerate(plans):
-                a, ss, mine, dev = plan[0], plan[4], plan[6], plan[8]
-                if b == BLOCKS - 1:
-                    start(ss.at[mine], ss.at[mine], s_send.at[p], s_recv.at[p], dev[k])
-                if b == BLOCKS - 1 or k != 1:
-                    start(a.at[mine, b], a.at[mine, b], a_send.at[p], a_recv.at[p, b], dev[k])
+                a, mine, dev = plan[0], plan[6], plan[8]
+                start(a.at[mine, b], a.at[mine, b], a_send.at[p], a_recv.at[p, b], dev[k])
+
+    def send_far(b):
+        phase(f"far{b}")
+        for p, plan in enumerate(plans):
+            a, mine, dev = plan[0], plan[6], plan[8]
+            start(a.at[mine, b], a.at[mine, b], a_send.at[p], a_recv.at[p, b], dev[1])
 
     def relay(b):
         phase(f"relay{b}")
@@ -297,7 +306,7 @@
     def product(b):
         for p, (a, w, o, dest, ss, so, _, _, dev, mine, peers, back) in enumerate(plans):
             phase(f"wait{b}{p}")
-            if b < BLOCKS - 1:
+            if b in RELAYED:
                 arrived(a.at[0, b], a_send.at[p], r_recv.at[p, b], dev[0])
             else:
                 arrived(a.at[pl.ds(0, 3), b], a_send.at[p], a_recv.at[p, b], dev[0])
@@ -331,9 +340,10 @@
     relay(1)
     all_weights()
     relay(2)
+    send_far(3)
     product(0)
+    squares()
     product(1)
-    squares()
     product(2)
     product(3)
 
@@ -355,12 +365,9 @@
             for k in range(3):
                 total = total + dest[peers[k], b].astype(F32)
             at = b * SPAN + p * HALF
-            ov[at : at + HALF, :] = (total * scale).astype(BF16)
-        rows = pl.ds(b * SPAN, SPAN)
-        pltpu.make_async_copy(ov.at[rows], out_ref.at[rows], out_sem.at[0]).start()
+            out_ref[at : at + HALF, :] = (total * scale).astype(BF16)
 
     phase("drain")
-    pltpu.make_async_copy(ov, out_ref, out_sem.at[0]).wait()
     remote(payload, carry, st_send.at[0], st_recv.at[0], other).wait_send()
     for p, (a, w, o, dest, ss, so, _, _, dev, _, _, back) in enumerate(plans):
         for ref, send, recv in (
@@ -383,8 +390,9 @@
         kernel,
         out_shape=jax.ShapeDtypeStruct((rows, COLS), BF16),
         in_specs=[hbm] * 9,
-        out_specs=pl.BlockSpec(memory_space=pl.ANY),
+        out_specs=pl.BlockSpec(memory_space=pltpu.VMEM),
         scratch_shapes=[
+            pltpu.VMEM((SIDE, SIDE, WIDE, COLS), BF16),
             pltpu.SMEM((2, 2, HEADS), F32),
             pltpu.SMEM((HEADS,), F32),
             pltpu.VMEM((1, WIDE), F32),
@@ -402,16 +410,14 @@
             *[pltpu.VMEM((BLOCKS, NST, WIDE), F32)] * 2,
             *[pltpu.VMEM((BLOCKS, NST, WIDE), BF16)] * 2,
             *[pltpu.VMEM((NST, WIDE), F32)] * 2,
-            pltpu.VMEM((rows, COLS), BF16),
-            dma((10,)),
+            dma((11,)),
             *[dma((2,))] * 4,
             *[dma((1,))] * 2,
             dma((2,)),
             dma((2, BLOCKS)),
-            dma((2, BLOCKS - 1)),
+            dma((2, BLOCKS)),
             *[dma((2,))] * 5,
             dma((2, BLOCKS)),
-            dma((1,)),
         ],
         compiler_params=pltpu.CompilerParams(
             collective_id=0, has_side_effects=True, vmem_limit_bytes=48 * 1024 * 1024

time: 29.5 us -> 29 us (0.983)
  Pallas kernels: 28.7 us -> 28.1 us
    pallas_call x1, Pallas kernels: 28.7 us -> 28.1 us  [body(): pl.pallas_call(kernel, out_shape=jax.ShapeDtypeStruct((rows, COLS), BF16)...]
where the time goes in v3:
time: 29 us; the launch traced here: 28.9 us
  Pallas kernels  28.1 us (97%)
  local copies, waits for them, and re-layouts  0.71 us (2%)
    pallas_call x1, Pallas kernels, body(): pl.pallas_call(kernel, out_shape=jax.ShapeDtypeStruct((rows, COLS), BF16)...  28.1 us
    unnamed x1, local copies, waits for them, and re-layouts  0.71 us

profile of v3, /device:TPU:32, one launch (start us, length us, event | category | flops | bytes accessed | tf_op | source)
XLA Modules:
  0.0 28.9 jit_solution(4575266106397239348)
XLA Ops:
  0.0 28.1 %encoder.1 = bf16[1024,128]{1,0:T(8,128)(2,1)S(1)} custom-call(bf16[1024,256]{1,0:T(8,128)(2,1)} %x_hbm.1, bf16[1024,256]{1,0:T(8,128)(2,1)} %z_hbm.1, bf16[2,1024,128]{2,1,0:T(8,128)(2,1)} %pf_hbm.1, bf16[2,1024,128]{2,1,0:T(8,128)(2,1)} %pb_hbm.1, f32[2,4,1024]{2,1,0:T(4,128)} %st_hbm.1, f32[2,2,4]{2,1,0:T(2,128)} %hp_hbm.1, f32[4]{0:T(128)} %skip_hbm.1, ...), custom_call_target="tpu_custom_call" | custom-call | tf_op jit(solution)/shard_map/encoder/pallas_call | solution.py:389
  28.2 0.7 %copy.11 = bf16[1024,128]{1,0:T(8,128)(2,1)} copy(bf16[1024,128]{1,0:T(8,128)(2,1)S(1)} %encoder.1) | data formatting | bytes 524288

commit v4 on v3

--- a/solution.py
+++ b/solution.py
@@ -117,7 +117,7 @@
     )
 
     half = pl.ds(2 * seq, 2)
-    for k in range(3):
+    for k in (1, 0, 2):
         start(wv.at[half, xs[k]], w1.at[half, :, tile(my_x)], w_send.at[0], w_recv.at[0], to_x[k])
         start(wv.at[ys[k], half], w2.at[half, :, tile(my_y)], w_send.at[1], w_recv.at[1], to_y[k])
 
@@ -315,7 +315,7 @@
             values = dot(lhs, w[...].reshape(SIDE * WIDE, SIDE * COLS)).astype(BF16)
             for j in range(SIDE):
                 o[b, j] = values[:, j * COLS : (j + 1) * COLS]
-            for k in range(3):
+            for k in (1, 0, 2):
                 start(o.at[b, peers[k]], dest.at[mine, b], o_send.at[p], o_recv.at[p, b], back[k])
 
     def squares():

time: 29 us -> 28.5 us (0.983)
  Pallas kernels: 28.1 us -> 27.8 us
    pallas_call x1, Pallas kernels: 28.1 us -> 27.8 us  [body(): pl.pallas_call(kernel, out_shape=jax.ShapeDtypeStruct((rows, COLS), BF16)...]
where the time goes in v4:
time: 28.5 us
  Pallas kernels  27.8 us (98%)
  local copies, waits for them, and re-layouts  0.71 us (2%)
    pallas_call x1, Pallas kernels, body(): pl.pallas_call(kernel, out_shape=jax.ShapeDtypeStruct((rows, COLS), BF16)...  27.8 us
    unnamed x1, local copies, waits for them, and re-layouts  0.71 us

profile of v4, /device:TPU:32, one launch (start us, length us, event | category | flops | bytes accessed | tf_op | source)
XLA Modules:
  0.0 28.5 jit_solution(9432530880160014818)
XLA Ops:
  0.0 27.8 %encoder.1 = bf16[1024,128]{1,0:T(8,128)(2,1)S(1)} custom-call(bf16[1024,256]{1,0:T(8,128)(2,1)} %x_hbm.1, bf16[1024,256]{1,0:T(8,128)(2,1)} %z_hbm.1, bf16[2,1024,128]{2,1,0:T(8,128)(2,1)} %pf_hbm.1, bf16[2,1024,128]{2,1,0:T(8,128)(2,1)} %pb_hbm.1, f32[2,4,1024]{2,1,0:T(4,128)} %st_hbm.1, f32[2,2,4]{2,1,0:T(2,128)} %hp_hbm.1, f32[4]{0:T(128)} %skip_hbm.1, ...), custom_call_target="tpu_custom_call" | custom-call | tf_op jit(solution)/shard_map/encoder/pallas_call | solution.py:389
  27.8 0.7 %copy.11 = bf16[1024,128]{1,0:T(8,128)(2,1)} copy(bf16[1024,128]{1,0:T(8,128)(2,1)S(1)} %encoder.1) | data formatting | bytes 524288

commit v5 on v4

--- a/solution.py
+++ b/solution.py
@@ -279,7 +279,7 @@
         ss1[my_y, b : b + 1, :] = sums[0:1, :HALF]
         ss2[my_x, b : b + 1, :] = sums[0:1, HALF:]
         if b == BLOCKS - 1:
-            for k in range(3):
+            for k in (1, 0, 2):
                 for p, plan in enumerate(plans):
                     ss, mine, dev = plan[4], plan[6], plan[8]
                     start(ss.at[mine], ss.at[mine], s_send.at[p], s_recv.at[p], dev[k])
@@ -323,7 +323,7 @@
         for p, (_, _, _, _, ss, so, _, _, dev, mine, _, back) in enumerate(plans):
             arrived(ss.at[pl.ds(0, 3)], s_send.at[p], s_recv.at[p], dev[0])
             so[mine] = ss[0] + ss[1] + ss[2] + ss[3]
-            for k in range(3):
+            for k in (1, 0, 2):
                 start(so.at[mine], so.at[mine], t_send.at[p], t_recv.at[p], back[k])
 
     intra(0)
@@ -415,7 +415,7 @@
             *[dma((1,))] * 2,
             dma((2,)),
             dma((2, BLOCKS)),
-            dma((2, BLOCKS)),
+            dma((2, BLOCKS - 1)),
             *[dma((2,))] * 5,
             dma((2, BLOCKS)),
         ],

time: 28.5 us -> 28.5 us (level)
  no operation moved by 1% of the time
where the time goes in v5:
time: 28.5 us
  Pallas kernels  27.7 us (97%)
  local copies, waits for them, and re-layouts  0.71 us (2%)
    pallas_call x1, Pallas kernels, body(): pl.pallas_call(kernel, out_shape=jax.ShapeDtypeStruct((rows, COLS), BF16)...  27.7 us
    unnamed x1, local copies, waits for them, and re-layouts  0.71 us

profile of v5, /device:TPU:32, one launch (start us, length us, event | category | flops | bytes accessed | tf_op | source)
XLA Modules:
  0.0 28.5 jit_solution(485041677690886495)
XLA Ops:
  0.0 27.7 %encoder.1 = bf16[1024,128]{1,0:T(8,128)(2,1)S(1)} custom-call(bf16[1024,256]{1,0:T(8,128)(2,1)} %x_hbm.1, bf16[1024,256]{1,0:T(8,128)(2,1)} %z_hbm.1, bf16[2,1024,128]{2,1,0:T(8,128)(2,1)} %pf_hbm.1, bf16[2,1024,128]{2,1,0:T(8,128)(2,1)} %pb_hbm.1, f32[2,4,1024]{2,1,0:T(4,128)} %st_hbm.1, f32[2,2,4]{2,1,0:T(2,128)} %hp_hbm.1, f32[4]{0:T(128)} %skip_hbm.1, ...), custom_call_target="tpu_custom_call" | custom-call | tf_op jit(solution)/shard_map/encoder/pallas_call | solution.py:389
  27.7 0.7 %copy.11 = bf16[1024,128]{1,0:T(8,128)(2,1)} copy(bf16[1024,128]{1,0:T(8,128)(2,1)S(1)} %encoder.1) | data formatting | bytes 524288
